TPU v7x, 32 devices: a whole 2x2x4 slice. The times are simulated.
32 devices in a mesh: rep: 4 (over z), exp: 4 (over x, core), shard: 2 (over y).
Axes of the slice: x: 2, y: 2, z: 4, core: 2. Of those that a mesh axis runs over, the one named last changes fastest.
Arguments:
- tokens: bfloat16 [3584, 2048], P(('rep', 'exp', 'shard')), may hold values from -1.5 to 1.5
- routes: int32 [3584, 2], P(('rep', 'exp', 'shard')), may hold values from 0 to 3, all different within a row; in each aligned block of 112 rows (0 to 111, 112 to 223, ...) at most 63 rows name the same one
- gate_weight: bfloat16 [4, 2048, 7168], P('exp', None, 'shard'), may hold values from -0.125 to 0.125
- gate_cotangent: bfloat16 [4, 2016, 7168], P('exp', 'rep', 'shard'), may hold values from -0.75 to 0.75
Outputs:
- token_grad: bfloat16 [3584, 2048], P(('rep', 'exp', 'shard'))
- weight_grad: bfloat16 [4, 2048, 7168], P('exp', None, 'shard')
Inputs may be any that keep to these rules, and one draw needn't show every extreme that they name: `routes`: the two entries of a row differ. The rows of one device name one expert at most 63 times, and some device names some expert exactly 63 times.
All inputs are finite; a program needn't handle non-finite values.
Results may differ from a plain program's by a relative error of at most 0.015.
Values may be sent and summed in bfloat16 or wider, within the bound.
A program may use at most 128 MiB of HBM per device.

v0:
```python
import jax
import jax.numpy as jnp
from jax import lax
from jax.sharding import PartitionSpec as P


def slot_matrix(route_rows, experts, slot_cap):
    expert_ids = jnp.arange(experts, dtype=jnp.int32)
    onehot = (route_rows[:, :, None] == expert_ids[None, None, :]).astype(jnp.int32)
    flattened = onehot.reshape(-1, experts)
    before = jnp.cumsum(flattened, axis=0) - flattened
    position = jnp.sum(before * flattened, axis=1)
    target = jnp.sum(flattened * expert_ids[None, :], axis=1) * slot_cap + position
    slot_ids = jnp.arange(experts * slot_cap, dtype=jnp.int32)
    matches = (target[None, :] == slot_ids[:, None]).astype(jnp.int32)
    return matches.reshape(experts * slot_cap, -1, 2).sum(axis=2)


def body(tokens, routes, gate_weight, gate_cotangent):
    experts = lax.axis_size("exp")
    shards = lax.axis_size("shard")
    features = tokens.shape[1]
    cotangent = gate_cotangent[0]
    hidden = cotangent.shape[1]
    slot_cap = cotangent.shape[0] // (experts * shards)
    weight = gate_weight[0]
    blocks = cotangent.reshape(experts, shards, slot_cap, hidden)
    placing = slot_matrix(routes, experts, slot_cap).astype(jnp.bfloat16)
    outgoing = jnp.dot(placing, tokens, preferred_element_type=jnp.float32).astype(jnp.bfloat16)
    outgoing = outgoing.reshape(experts, slot_cap, features)
    contract_rows = (((0,), (0,)), ((), ()))
    copies = jnp.broadcast_to(outgoing[:, None], (experts, shards, slot_cap, features))
    copies = copies.reshape(experts * shards, slot_cap, features)
    arrived = lax.all_to_all(copies, ("exp", "shard"), split_axis=0, concat_axis=0, tiled=True)
    partial_grad = lax.dot_general(
        arrived.reshape(-1, features), cotangent, contract_rows, preferred_element_type=jnp.float32
    )
    weight_grad = lax.psum(partial_grad.astype(jnp.bfloat16), "rep")[None]
    ordered = jnp.swapaxes(blocks, 0, 1).reshape(-1, hidden)
    summed = lax.psum_scatter(
        lax.dot_general(
            ordered, weight, (((1,), (1,)), ((), ())), preferred_element_type=jnp.float32
        ).astype(jnp.bfloat16),
        "shard",
        scatter_dimension=0,
        tiled=True,
    )
    slot_grad = summed.reshape(experts, slot_cap, features)
    returned = lax.all_to_all(slot_grad, "exp", split_axis=0, concat_axis=0, tiled=True)
    token_grad = jnp.dot(
        placing.T, returned.reshape(-1, features), preferred_element_type=jnp.float32
    )
    return (token_grad.astype(jnp.bfloat16), weight_grad)


def solution(mesh):
    placed = (
        P(("rep", "exp", "shard"), None),
        P(("rep", "exp", "shard"), None),
        P("exp", None, "shard"),
        P("exp", "rep", "shard"),
    )
    return jax.shard_map(
        body,
        mesh=mesh,
        in_specs=placed,
        out_specs=(P(("rep", "exp", "shard"), None), P("exp", None, "shard")),
        check_vma=False,
    )
```

profile of v0, /device:TPU:0, one launch (start us, length us, event | category | flops | bytes accessed | tf_op | source)
XLA Modules:
  0.0 571.3 jit_solution(2415380312625847076)
XLA Ops:
  7.2 0.8 copy.16
  8.2 1.2 reduce-window.6
  10.2 0.5 convolution_convert_fusion.1
  10.7 0.3 broadcast_in_dim.6
  11.0 0.2 broadcast_in_dim.7
  11.2 30.7 %all_to_all.10 = bf16[8,63,2048]{2,1,0:T(8,128)(2,1)S(1)} all-to-all(bf16[8,63,2048]{2,1,0:T(8,128)(2,1)S(1)} %bitcast.29), channel_id=1, replica_groups=mesh['rep'=4,'exp'=4,'shard'=2] {'exp','shard'}, dimensions={0} | all-to-all | bytes 4128768 | tf_op jit(solution)/shard_map/all_to_all | solution.py:34
  41.9 2.0 reshape.61
  43.8 13.3 %fusion.3 = bf16[1,2048,3584]{2,1,0:T(8,128)(2,1)} fusion(bf16[504,2048]{1,0:T(8,128)(2,1)} %reshape.61, bf16[1,504,3584]{2,1,0:T(8,128)(2,1)} %param.7), kind=kOutput, calls=%fused_computation.3 | convolution fusion | flops 7406092288 | bytes 20357120 | tf_op jit(solution)/shard_map/dot_general | solution.py:35
  57.2 4.9 reshape_squeeze.3
  62.1 5.2 copy.20
  67.2 4.9 reshape.57
  72.2 13.0 %fusion.5 = bf16[504,2048]{1,0:T(8,128)(2,1)} fusion(bf16[504,3584]{1,0:T(8,128)(2,1)} %reshape.57, bf16[1,2048,3584]{2,1,0:T(8,128)(2,1)} %param.6), kind=kOutput, calls=%fused_computation.5 | convolution fusion | flops 7399784448 | bytes 20357120 | tf_op jit(solution)/shard_map/dot_general | solution.py:41
  85.2 28.6 %fusion = bf16[256,2048]{1,0:T(8,128)(2,1)S(1)} fusion(bf16[504,2048]{1,0:T(8,128)(2,1)} %fusion.5), kind=kCustom, calls=%all-reduce-scatter | all-reduce-scatter fusion | flops 1048577 | bytes 3113472
  113.8 3.6 collective-permute-start
  117.5 0.6 dynamic-slice.4
  118.7 0.2 collective-permute-done
  118.9 1.2 concatenate
  120.1 0.3 constant_dynamic-slice_fusion
  120.4 0.3 reshape.58
  120.7 17.6 %all_to_all.11 = bf16[4,63,2048]{2,1,0:T(8,128)(2,1)} all-to-all(bf16[4,63,2048]{2,1,0:T(8,128)(2,1)S(1)} %reshape.58), channel_id=1, replica_groups=mesh['rep'=4,'exp'=4,'shard'=2] {'exp'}, dimensions={0} | all-to-all | bytes 2064384 | tf_op jit(solution)/shard_map/all_to_all | solution.py:49
  138.3 1.5 reshape.59
  139.8 1.1 convolution_convert_fusion.2
  140.9 410.5 %all-reduce.5.cloned.1.call-done = bf16[1,2048,3584]{2,1,0:T(8,128)(2,1)} async-done(((bf16[1,2048,3584]{2,1,0:T(8,128)(2,1)}), bf16[1,2048,3584]{2,1,0:T(8,128)(2,1)}) %all-reduce.5.cloned.1.call-update) | async-done | bytes 14680080 | tf_op jit(solution)/shard_map/psum | solution.py:38
  551.3 13.2 %copy.25 = bf16[1,2048,3584]{2,1,0:T(8,128)(2,1)} copy(bf16[1,2048,3584]{2,1,0:T(8,128)(2,1)} %all-reduce.5.cloned.1.call-done) | data formatting | bytes 29360128
  (25 shorter events, 1.0 us)
Async XLA Ops:
  7.2 3.1 copy-start
  7.2 544.1 %all-reduce.5.cloned.1.call-start = ((), (), s32[]{:S(2)}) async-start(), calls=%async_computation.2 | async-start | bytes 29360128 | tf_op jit(solution)/shard_map/psum | solution.py:38
  72.2 45.3 %copy-start.2 = (u32[32]{0:T(128)S(1)}, u32[32]{0:T(128)}, u32[]{:S(2)}) copy-start(u32[32]{0:T(128)} %constant.19) | copy-start | bytes 388
  113.8 5.1 collective-permute-start
  551.3 13.2 %copy-start.1 = (bf16[112,2048]{1,0:T(8,128)(2,1)S(1)}, bf16[112,2048]{1,0:T(8,128)(2,1)}, u32[]{:S(2)}) copy-start(bf16[112,2048]{1,0:T(8,128)(2,1)} %param.4) | copy-start | bytes 1376260
Sparse Core Ops, SparseCore 0:
  57.3 493.9 all-reduce.4
where the time goes:
time: 572 us; the launch traced here: 571 us
  waiting for transfers between devices  411 us (72%)
  blocking collectives  76.8 us (13%)
  local copies, waits for them, and re-layouts  36 us (6%)
  matrix products  27.9 us (5%)
  between operations  14.8 us (3%)
    psum x1, waiting for transfers between devices, body(): weight_grad = lax.psum(partial_grad.astype(jnp.bfloat16), 'rep')[None]  410 us
    all_to_all x1, blocking collectives, body(): lax.all_to_all(copies, ('exp', 'shard'), split_axis=0, concat_axis=0, til...  30.7 us
    unnamed x1, blocking collectives  28.6 us
    all_to_all x1, blocking collectives, body(): lax.all_to_all(slot_grad, 'exp', split_axis=0, concat_axis=0, tiled=True)  17.6 us
    unnamed x13, local copies, waits for them, and re-layouts  16.1 us
    dot_general x1, matrix products, body(): lax.dot_general(arrived.reshape(-1, features), cotangent, contract_rows,...  13.3 us
    dot_general x1, matrix products, body(): lax.dot_general(ordered, weight, (((1,), (1,)), ((), ())), preferred_elem...  13 us
  transfers between devices with their start and end apart: 2, of which 2 were waited for; matrix products, arithmetic and copies ran while one was open for 11% of the time, Pallas kernels for 0%

commit v1 on v0

--- a/solution.py
+++ b/solution.py
@@ -35,7 +35,7 @@
     partial_grad = lax.dot_general(
         arrived.reshape(-1, features), cotangent, contract_rows, preferred_element_type=jnp.float32
     )
-    weight_grad = lax.psum(partial_grad.astype(jnp.bfloat16), "rep")[None]
+    weight_grad = jnp.sum(lax.all_gather(partial_grad.astype(jnp.bfloat16), "rep"), axis=0)[None]
     ordered = jnp.swapaxes(blocks, 0, 1).reshape(-1, hidden)
     summed = lax.psum_scatter(
         lax.dot_general(

time: 572 us -> 1070 us (1.87)
  waiting for transfers between devices: 411 us -> 886 us
  other arithmetic: 1.5 us -> 29.1 us
  local copies, waits for them, and re-layouts: 36 us -> 24.8 us
    all_gather x0 -> x1, waiting for transfers between devices: none -> 886 us  [body(): lax.all_gather(partial_grad.astype(jnp.bfloat16), 'rep')]
    psum x1 -> x0, waiting for transfers between devices: 410 us -> none  [body(): weight_grad = lax.psum(partial_grad.astype(jnp.bfloat16), 'rep')[None]]
    reduce_sum x0 -> x1, other arithmetic: none -> 27.6 us  [body(): jnp.sum(lax.all_gather(partial_grad.astype(jnp.bfloat16), 'rep'), axis=0)]
    unnamed x13 -> x12, local copies, waits for them, and re-layouts: 16.1 us -> 2.95 us
  transfers between devices with their start and end apart: 2 -> 2, of which waited for: 2 -> 1; matrix products, arithmetic and copies ran while one was open for 11% -> 6% of each run, Pallas kernels for 0% -> 0%
where the time goes in v1:
time: 1070 us
  waiting for transfers between devices  886 us (83%)
  blocking collectives  77.2 us (7%)
  matrix products  30.9 us (3%)
  other arithmetic  29.1 us (3%)
  local copies, waits for them, and re-layouts  24.8 us (2%)
  between operations  14.8 us (1%)
    all_gather x1, waiting for transfers between devices, body(): lax.all_gather(partial_grad.astype(jnp.bfloat16), 'rep')  886 us
    all_to_all x1, blocking collectives, body(): lax.all_to_all(copies, ('exp', 'shard'), split_axis=0, concat_axis=0, til...  30.7 us
    unnamed x1, blocking collectives  28.9 us
    reduce_sum x1, other arithmetic, body(): jnp.sum(lax.all_gather(partial_grad.astype(jnp.bfloat16), 'rep'), axis=0)  27.6 us
  transfers between devices with their start and end apart: 2, of which 1 were waited for; matrix products, arithmetic and copies ran while one was open for 6% of the time, Pallas kernels for 0%

profile of v1, /device:TPU:0, one launch (start us, length us, event | category | flops | bytes accessed | tf_op | source)
XLA Modules:
  0.0 1066.4 jit_solution(10015116792229170456)
XLA Ops:
  7.2 0.8 copy.16
  8.1 0.1 eq.37
  8.2 1.2 reduce-window.6
  10.2 0.5 convolution_convert_fusion.1
  10.7 0.3 broadcast_in_dim.6
  11.0 0.2 broadcast_in_dim.7
  11.2 30.7 %all_to_all.10 = bf16[8,63,2048]{2,1,0:T(8,128)(2,1)S(1)} all-to-all(bf16[8,63,2048]{2,1,0:T(8,128)(2,1)S(1)} %bitcast.31), channel_id=1, replica_groups=mesh['rep'=4,'exp'=4,'shard'=2] {'exp','shard'}, dimensions={0} | all-to-all | bytes 4128768 | tf_op jit(solution)/shard_map/all_to_all | solution.py:34
  41.9 2.0 reshape.61
  43.8 13.3 %convolution_convert_fusion = bf16[2048,3584]{1,0:T(8,128)(2,1)} fusion(bf16[504,2048]{1,0:T(8,128)(2,1)} %reshape.61, bf16[1,504,3584]{2,1,0:T(8,128)(2,1)} %param.7), kind=kOutput, calls=%fused_computation | convolution fusion | flops 7406092288 | bytes 20357120 | tf_op jit(solution)/shard_map/dot_general | solution.py:35
  57.2 4.9 reshape_squeeze.3
  62.1 4.7 copy.20
  66.8 7.3 reshape.57
  74.1 16.1 %fusion.4 = bf16[504,2048]{1,0:T(8,128)(2,1)} fusion(bf16[504,3584]{1,0:T(8,128)(2,1)} %reshape.57, bf16[1,2048,3584]{2,1,0:T(8,128)(2,1)} %param.6), kind=kOutput, calls=%fused_computation.4 | convolution fusion | flops 7399784448 | bytes 20357120 | tf_op jit(solution)/shard_map/dot_general | solution.py:41
  90.2 28.9 %fusion = bf16[256,2048]{1,0:T(8,128)(2,1)S(1)} fusion(bf16[504,2048]{1,0:T(8,128)(2,1)} %fusion.4), kind=kCustom, calls=%all-reduce-scatter | all-reduce-scatter fusion | flops 1048577 | bytes 3113472
  119.2 3.7 collective-permute-start
  122.9 0.6 dynamic-slice.4
  124.2 1.2 concatenate
  125.4 0.3 constant_dynamic-slice_fusion
  125.7 0.3 reshape.58
  126.0 17.6 %all_to_all.11 = bf16[4,63,2048]{2,1,0:T(8,128)(2,1)} all-to-all(bf16[4,63,2048]{2,1,0:T(8,128)(2,1)S(1)} %reshape.58), channel_id=1, replica_groups=mesh['rep'=4,'exp'=4,'shard'=2] {'exp'}, dimensions={0} | all-to-all | bytes 2064384 | tf_op jit(solution)/shard_map/all_to_all | solution.py:49
  143.5 1.5 reshape.59
  145.1 1.1 convolution_convert_fusion.2
  146.1 885.8 %all-gather.3.cloned.1.call-done = bf16[8192,3584]{1,0:T(8,128)(2,1)} async-done(((bf16[2048,3584]{1,0:T(8,128)(2,1)}), bf16[8192,3584]{1,0:T(8,128)(2,1)}) %all-gather.3.cloned.1.call-update) | async-done | bytes 58720272 | tf_op jit(solution)/shard_map/all_gather | solution.py:38
  1032.0 27.6 %reduce_sum.42 = bf16[2048,3584]{1,0:T(8,128)(2,1)} reduce(bf16[4,2048,3584]{2,1,0:T(8,128)(2,1)} %bitcast.28, bf16[]{:T(256)} %constant.13.clone.1), dimensions={0}, to_apply=%region_6.7 | reduce | flops 22020096 | bytes 73400320 | tf_op jit(solution)/shard_map/reduce_sum | solution.py:38
  (25 shorter events, 0.9 us)
Async XLA Ops:
  7.2 3.1 copy-start
  7.2 1024.8 %all-gather.3.cloned.1.call-start = ((), (), s32[]{:S(2)}) async-start(), calls=%async_computation.2 | async-start | bytes 73400320 | tf_op jit(solution)/shard_map/all_gather | solution.py:38
  74.1 48.8 %copy-start.2 = (u32[32]{0:T(128)S(1)}, u32[32]{0:T(128)}, u32[]{:S(2)}) copy-start(u32[32]{0:T(128)} %constant.22) | copy-start | bytes 388
  119.2 5.0 collective-permute-start
  1032.0 27.6 %copy-start.1 = (bf16[112,2048]{1,0:T(8,128)(2,1)S(1)}, bf16[112,2048]{1,0:T(8,128)(2,1)}, u32[]{:S(2)}) copy-start(bf16[112,2048]{1,0:T(8,128)(2,1)} %param.4) | copy-start | bytes 1376260
Sparse Core Ops, SparseCore 0:
  57.3 974.6 all-gather.2
